TPU v7x, 512 devices: a whole 4x4x16 slice. The times are simulated.
512 devices in a mesh: ctx: 128 (over z, x, y_hi), head: 4 (over y_lo, core).
Axes of the slice: x: 4, y: 4 (y_hi: 2, y_lo: 2; y = y_hi * 2 + y_lo), z: 16, core: 2. Of those that a mesh axis runs over, the one named last changes fastest.
Arguments:
- queries: bfloat16 [8192, 8192], P('ctx', 'head'), may hold values from -6 to 6
- keys: bfloat16 [8192, 128], P('ctx'), may hold values from -6 to 6
- key_gain: float32 [128], replicated, may hold values from 0.25 to 1.75
- key_bias: float32 [128], replicated, may hold values from -0.5 to 0.5
- head_weights: bfloat16 [8192, 64], P('ctx', 'head'), may hold values from -6 to 6
- positions: int32 [8192], P('ctx'), may hold values from 0 to 6143, as said below
Outputs:
- index_scores: float32 [8192, 8192], P(('ctx', 'head'))
Inputs may be any that keep to these rules, and one draw needn't show every extreme that they name: `positions`: positions of packed documents: the first 6144 tokens form one document and the rest is split into one to three documents at drawn points; a token's position counts from its document's first token.
All inputs are finite; a program needn't handle non-finite values.
Results may differ from a plain program's by a relative error of at most 0.0095.
Values may be sent and summed in bfloat16 or wider, within the bound.
No kernel may reach another device: no remote copies, remote signals or barrier semaphores. Data moves between devices by JAX's collectives and lax.ppermute only.
A program may use at most 64 MiB of HBM per device.

v0:
```python
import math
import jax
import jax.numpy as jnp
import numpy as np
from jax import lax
from jax.sharding import PartitionSpec as P

H = 64
DH = 128
ROPE = 64


def yarn_frequencies(rope_dims):
    half_dims = rope_dims // 2
    exponent = np.arange(0, rope_dims, 2) / rope_dims
    extra_freq = 1.0 / 10000.0**exponent
    inter_freq = extra_freq / 40.0

    def correction(beta):
        return rope_dims * math.log(4096.0 / (beta * 2.0 * math.pi)) / (2.0 * math.log(10000.0))

    low_dim = max(math.floor(correction(32.0)), 0)
    high_dim = min(math.ceil(correction(1.0)), rope_dims - 1)
    ramp_values = np.clip((np.arange(half_dims) - low_dim) / (high_dim - low_dim), 0.0, 1.0)
    return (inter_freq * ramp_values + extra_freq * (1.0 - ramp_values)).astype(np.float32)


def rotate(values, angles):
    half_rope = ROPE // 2
    cosine = jnp.cos(angles)[:, None, :]
    sine = jnp.sin(angles)[:, None, :]
    first = values[..., :half_rope]
    second = values[..., half_rope:ROPE]
    return jnp.concatenate(
        [first * cosine - second * sine, second * cosine + first * sine, values[..., ROPE:]], -1
    )


def key_norm(keys, key_gain, key_bias):
    values = keys.astype(jnp.float32)
    centered = values - jnp.mean(values, axis=-1, keepdims=True)
    spread = jnp.mean(centered * centered, axis=-1, keepdims=True)
    return centered * lax.rsqrt(spread + 1e-06) * key_gain + key_bias


def tile_scores(q_block, weights, k_block, groups, row_glob, row_doc, key_glob):
    rows_here = q_block.shape[0]
    heads_here = weights.shape[1]
    raw = lax.dot_general(
        q_block.reshape(rows_here * heads_here, DH),
        k_block,
        (((1,), (1,)), ((), ())),
        preferred_element_type=jnp.float32,
    )
    active = jnp.maximum(raw, 0.0).reshape(
        rows_here, groups, heads_here // groups, k_block.shape[0]
    )
    partial_sum = jnp.sum(
        active * weights.reshape(rows_here, groups, heads_here // groups, 1), axis=2
    )
    visible = (key_glob[None, :] >= row_doc[:, None]) & (key_glob[None, :] <= row_glob[:, None])
    partial_sum = jnp.where(visible[:, None, :], partial_sum, jnp.zeros_like(partial_sum))
    return partial_sum.astype(jnp.bfloat16)


def on_device(queries, keys, key_gain, key_bias, head_weights, positions):
    tok_rows = queries.shape[0]
    local_heads = queries.shape[1] // DH
    ctx_rank = lax.axis_index("ctx")
    freqs = jnp.asarray(yarn_frequencies(ROPE))
    angles = positions.astype(jnp.float32)[:, None] * freqs[None, :]
    q_rot = (
        rotate(queries.astype(jnp.float32).reshape(tok_rows, local_heads, DH), angles)
        .reshape(tok_rows, local_heads * DH)
        .astype(jnp.bfloat16)
    )
    k_rot = (
        rotate(key_norm(keys, key_gain, key_bias)[:, None, :], angles)
        .reshape(tok_rows, DH)
        .astype(jnp.bfloat16)
    )
    scale = 1.0 / math.sqrt(H * DH)
    groups = 1
    rows_w = head_weights.astype(jnp.float32) * scale
    row_glob = ctx_rank * tok_rows + jnp.arange(tok_rows, dtype=jnp.int32)
    row_doc = row_glob - positions
    rows_here = q_rot.shape[0]
    out_type = jnp.bfloat16
    row_last = jnp.max(row_glob)
    doc_first = jnp.min(row_doc)

    def score_block(k_block, key_glob):
        parts = tile_scores(q_rot, rows_w, k_block, groups, row_glob, row_doc, key_glob)
        return parts[:, 0, :]

    piece = lax.all_gather(k_rot, "ctx", axis=0, tiled=True)
    start = jnp.int32(0)
    piece_len = piece.shape[0]
    block_len = math.gcd(piece_len, 512)
    count = piece_len // block_len

    def compute(operand):
        stacked = piece.reshape(count, block_len, DH)
        offsets = block_len * jnp.arange(count, dtype=jnp.int32)

        def one_block(inputs):
            k_block, offset = inputs
            return score_block(k_block, offset + jnp.arange(block_len, dtype=jnp.int32))

        tiles = lax.map(one_block, (stacked, offsets))
        return jnp.transpose(tiles, (1, 0, 2)).reshape(rows_here, piece_len)

    def skip(operand):
        return jnp.zeros((rows_here, piece_len), out_type)

    live = (start <= row_last) & (start + piece_len > doc_first)
    partials = lax.cond(live, compute, skip, 0)
    return lax.psum_scatter(partials, "head", scatter_dimension=0, tiled=True).astype(jnp.float32)


def solution(mesh):
    in_specs = (P("ctx", "head"), P("ctx", None), P(), P(), P("ctx", "head"), P("ctx"))
    out_specs = P(("ctx", "head"), None)
    return jax.shard_map(
        on_device, mesh=mesh, in_specs=in_specs, out_specs=out_specs, check_vma=False
    )
```

profile of v0, /device:TPU:1, one launch (start us, length us, event | category | flops | bytes accessed | tf_op | source)
XLA Modules:
  0.0 366.6 jit_solution(11451459381095986542)
XLA Ops:
  6.5 0.8 copy.20
  7.5 0.8 fusion.10
  8.3 1.4 fusion.21
  9.7 0.8 fusion.16
  10.5 0.7 copy.21
  11.3 1.0 convert_bitcast_fusion
  14.6 207.3 %all-gather.3.cloned.1.call-done = bf16[8192,1,128]{2,0,1:T(8,128)(2,1)} async-done(((bf16[64,1,128]{2,0,1:T(8,128)(2,1)}), bf16[8192,1,128]{2,0,1:T(8,128)(2,1)}) %all-gather.3.cloned.1.call-update) | async-done | bytes 2097168 | tf_op jit(solution)/shard_map/all_gather | solution.py:96
  221.9 102.7 %conditional.1 = (bf16[64,8192]{1,0:T(8,128)(2,1)S(1)}) conditional(s32[]{:T(128)} %convert_element_type.40, () %tuple.18, (bf16[8192,128]{1,0:T(8,128)(2,1)}, bf16[64,16,128]{2,1,0:T(8,128)(2,1)S(1)}, f32[64,16]{1,0:T(8,128)S(1)}, s32[64]{0:T(128)S(1)}, s32[64]{0:T(128)S(1)}) %tuple.49), branch_computations={%region_4.0_spmd, %region_5.9_spmd} | conditional | flops 135890448 | bytes 13190965 | solution.py:117
  222.6 101.8 %while.13 = (s32[]{:T(128)}, bf16[16,64,512]{2,1,0:T(8,128)(2,1)S(1)}, s32[16]{0:T(128)S(1)}, s32[64]{0:T(128)S(1)}, s32[64]{0:T(128)S(1)}, /*index=5*/bf16[16,5...) while((s32[]{:T(128)}, ...), condition=%wide.wide.region_8.8_spmd, body=%wide.wide.region_6.7_spmd.sunk | while | flops 135889408 | bytes 8988281 | solution.py:110
  222.6 2.6 maximum_bitcast_fusion.3
  225.3 1.9 copy.30
  227.7 0.6 dynamic_slice.17
  228.3 0.6 iota_add_fusion.4
  229.0 2.6 maximum_bitcast_fusion.3
  231.6 1.9 copy.30
  234.0 0.6 dynamic_slice.17
  234.6 0.6 iota_add_fusion.4
  235.4 2.6 maximum_bitcast_fusion.3
  238.0 1.9 copy.30
  240.4 0.6 dynamic_slice.17
  241.0 0.6 iota_add_fusion.4
  241.7 2.6 maximum_bitcast_fusion.3
  244.4 1.9 copy.30
  247.4 0.6 iota_add_fusion.4
  248.1 2.6 maximum_bitcast_fusion.3
  250.7 1.9 copy.30
  253.7 0.6 iota_add_fusion.4
  254.5 2.6 maximum_bitcast_fusion.3
  257.1 1.9 copy.30
  260.1 0.6 iota_add_fusion.4
  260.8 2.6 maximum_bitcast_fusion.3
  263.5 1.9 copy.30
  266.5 0.6 iota_add_fusion.4
  267.2 2.6 maximum_bitcast_fusion.3
  269.8 1.9 copy.30
  272.8 0.6 iota_add_fusion.4
  273.6 2.6 maximum_bitcast_fusion.3
  276.2 1.9 copy.30
  279.2 0.6 iota_add_fusion.4
  279.9 2.6 maximum_bitcast_fusion.3
  282.6 1.9 copy.30
  285.6 0.6 iota_add_fusion.4
  286.3 2.6 maximum_bitcast_fusion.3
  288.9 1.9 copy.30
  291.9 0.6 iota_add_fusion.4
  292.7 2.6 maximum_bitcast_fusion.3
  295.3 1.9 copy.30
  298.3 0.6 iota_add_fusion.4
  299.0 2.6 maximum_bitcast_fusion.3
  301.7 1.9 copy.30
  304.7 0.6 iota_add_fusion.4
  305.4 2.6 maximum_bitcast_fusion.3
  308.0 1.9 copy.30
  311.0 0.6 iota_add_fusion.4
  311.8 2.6 maximum_bitcast_fusion.3
  314.4 1.9 copy.30
  317.4 0.6 iota_add_fusion.4
  318.1 2.6 maximum_bitcast_fusion.3
  320.8 1.9 copy.30
  323.2 0.6 dynamic_slice.17
  323.8 0.6 iota_add_fusion.4
  324.6 1.0 copy-done
  325.6 32.4 %reduce-scatter.2.cloned.1.call-done = bf16[16,8192]{1,0:T(8,128)(2,1)} async-done(((bf16[64,8192]{1,0:T(8,128)(2,1)}), bf16[16,8192]{1,0:T(8,128)(2,1)}) %reduce-scatter.2.cloned.1.call-update) | async-done | bytes 262160 | tf_op jit(solution)/shard_map/reduce_scatter | solution.py:118
  358.0 1.8 convert_element_type.45
  (75 shorter events, 18.1 us)
Async XLA Ops:
  6.5 7.4 %copy-start.3 = (f32[32]{0:T(128)S(1)}, f32[32]{0:T(128)}, u32[]{:S(2)}) copy-start(f32[32]{0:T(128)} %constant.54.clone) | copy-start | bytes 388
  6.5 6.0 %copy-start.2 = (bf16[64,16]{0,1:T(8,128)(2,1)S(1)}, bf16[64,16]{0,1:T(8,128)(2,1)}, u32[]{:S(2)}) copy-start(bf16[64,16]{0,1:T(8,128)(2,1)} %param.15) | copy-start | bytes 6148
  6.5 215.3 %all-gather.3.cloned.1.call-start = ((), (), s32[]{:S(2)}) async-start(), calls=%async_computation.2 | async-start | bytes 2113536 | tf_op jit(solution)/shard_map/all_gather | solution.py:96
  11.2 346.8 %reduce-scatter.2.cloned.1.call-start = ((), (), s32[]{:S(2)}) async-start(), calls=%async_computation.1 | async-start | bytes 1310720 | tf_op jit(solution)/shard_map/reduce_scatter | solution.py:118
  221.9 0.7 copy-start.1
  324.6 1.0 copy-start
Sparse Core Ops, SparseCore 0:
  11.8 209.9 all-gather.2
  325.7 32.2 reduce-scatter.1
where the time goes:
time: 368 us; the launch traced here: 367 us
  waiting for transfers between devices  240 us (65%)
  local copies, waits for them, and re-layouts  44 us (12%)
  matrix products  42.2 us (11%)
  other arithmetic  25.3 us (7%)
  between operations  14.7 us (4%)
    all_gather x1, waiting for transfers between devices, on_device(): piece = lax.all_gather(k_rot, 'ctx', axis=0, tiled=True)  207 us
    dot_general x16, matrix products, tile_scores(): lax.dot_general(q_block.reshape(rows_here * heads_here, DH), k_block, (((...  42.2 us
    reduce_scatter x1, waiting for transfers between devices, on_device(): lax.psum_scatter(partials, 'head', scatter_dimension=0, tiled=True)  32.4 us
    max x16, local copies, waits for them, and re-layouts, tile_scores(): jnp.maximum(raw, 0.0)  30.7 us
    add x16, other arithmetic, one_block(): return score_block(k_block, offset + jnp.arange(block_len, dtype=jnp.int32))  9.88 us
    dynamic_slice x16, local copies, waits for them, and re-layouts, compute(): tiles = lax.map(one_block, (stacked, offsets))  9.55 us
    reduce_sum x16, other arithmetic, tile_scores(): jnp.sum(active * weights.reshape(rows_here, groups, heads_here // groups,...  7.39 us
  transfers between devices with their start and end apart: 2, of which 2 were waited for; matrix products, arithmetic and copies ran while one was open for 1% of the time, Pallas kernels for 0%

commit v1 on v0

--- a/solution.py
+++ b/solution.py
@@ -8,6 +8,13 @@
 H = 64
 DH = 128
 ROPE = 64
+
+
+def swapped_in(value, axis, along):
+    size = lax.axis_size(axis)
+    tiles = jnp.stack([value for _ in range(size)])
+    tiles = lax.all_to_all(tiles, axis, split_axis=0, concat_axis=0)
+    return jnp.concatenate(tiles, axis=along)
 
 
 def yarn_frequencies(rope_dims):
@@ -93,7 +100,7 @@
         parts = tile_scores(q_rot, rows_w, k_block, groups, row_glob, row_doc, key_glob)
         return parts[:, 0, :]
 
-    piece = lax.all_gather(k_rot, "ctx", axis=0, tiled=True)
+    piece = swapped_in(k_rot, "ctx", 0)
     start = jnp.int32(0)
     piece_len = piece.shape[0]
     block_len = math.gcd(piece_len, 512)

time: 368 us -> 269 us (0.73)
  waiting for transfers between devices: 240 us -> 116 us
  starting transfers between devices: 0.04 us -> 23.7 us
    all_gather x1 -> x0, waiting for transfers between devices: 207 us -> none  [on_device(): piece = lax.all_gather(k_rot, 'ctx', axis=0, tiled=True)]
    all_to_all x0 -> x1, waiting for transfers between devices: none -> 90.2 us  [swapped_in(): tiles = lax.all_to_all(tiles, axis, split_axis=0, concat_axis=0)]
    all_to_all x0 -> x1, starting transfers between devices: none -> 23.6 us  [swapped_in(): tiles = lax.all_to_all(tiles, axis, split_axis=0, concat_axis=0)]
    reduce_scatter x1, waiting for transfers between devices: 32.4 us -> 26.1 us  [on_device(): lax.psum_scatter(partials, 'head', scatter_dimension=0, tiled=True)]
  transfers between devices with their start and end apart: 2 -> 2, of which waited for: 2 -> 2; matrix products, arithmetic and copies ran while one was open for 1% -> 0% of each run, Pallas kernels for 0% -> 0%
where the time goes in v1:
time: 269 us; the launch traced here: 267 us
  waiting for transfers between devices  116 us (43%)
  local copies, waits for them, and re-layouts  45.5 us (17%)
  matrix products  42.2 us (16%)
  other arithmetic  24.3 us (9%)
  starting transfers between devices  23.7 us (9%)
  between operations  14.8 us (6%)
    all_to_all x1, waiting for transfers between devices, swapped_in(): tiles = lax.all_to_all(tiles, axis, split_axis=0, concat_axis=0)  90.2 us
    dot_general x16, matrix products, tile_scores(): lax.dot_general(q_block.reshape(rows_here * heads_here, DH), k_block, (((...  42.2 us
    max x16, local copies, waits for them, and re-layouts, tile_scores(): jnp.maximum(raw, 0.0)  30.7 us
    reduce_scatter x1, waiting for transfers between devices, on_device(): lax.psum_scatter(partials, 'head', scatter_dimension=0, tiled=True)  26.1 us
    all_to_all x1, starting transfers between devices, swapped_in(): tiles = lax.all_to_all(tiles, axis, split_axis=0, concat_axis=0)  23.6 us
    add x16, other arithmetic, one_block(): return score_block(k_block, offset + jnp.arange(block_len, dtype=jnp.int32))  9.88 us
    dynamic_slice x16, local copies, waits for them, and re-layouts, compute(): tiles = lax.map(one_block, (stacked, offsets))  9.55 us
    reduce_sum x16, other arithmetic, tile_scores(): jnp.sum(active * weights.reshape(rows_here, groups, heads_here // groups,...  7.39 us
  transfers between devices with their start and end apart: 2, of which 2 were waited for; matrix products, arithmetic and copies ran while one was open for 0% of the time, Pallas kernels for 0%

profile of v1, /device:TPU:1, one launch (start us, length us, event | category | flops | bytes accessed | tf_op | source)
XLA Modules:
  0.0 267.5 jit_solution(9604627888449642586)
XLA Ops:
  6.5 0.8 copy.15
  7.5 0.8 fusion.10
  8.3 1.4 fusion.21
  9.6 0.8 fusion.16
  10.5 1.8 stack.2
  12.4 23.6 %all-to-all-start = ((bf16[128,64,128]{2,1,0:T(8,128)(2,1)}), bf16[128,64,128]{2,1,0:T(8,128)(2,1)}, u32[]{:S(2)}, u32[]{:S(2)}) async-start(bf16[128,64,128]{2,1,0:T(8,128)(2,1)} %stack.2), calls=%async_computation | async-start | bytes 4194304 | tf_op jit(solution)/shard_map/all_to_all | solution.py:16
  38.8 90.2 %all-to-all-done = bf16[128,64,128]{2,1,0:T(8,128)(2,1)} async-done(((bf16[128,64,128]{2,1,0:T(8,128)(2,1)}), bf16[128,64,128]{2,1,0:T(8,128)(2,1)}, u32[]{:S(2)}, u32[]{:S(2)}) %all-to-all-start) | async-done | bytes 2097184 | tf_op jit(solution)/shard_map/all_to_all | solution.py:16
  129.0 102.7 %conditional.1 = (bf16[64,8192]{1,0:T(8,128)(2,1)S(1)}) conditional(s32[]{:T(128)} %convert_element_type.42, () %tuple.18, (bf16[128,64,128]{2,1,0:T(8,128)(2,1)}, bf16[64,16,128]{2,1,0:T(8,128)(2,1)S(1)}, f32[64,16]{1,0:T(8,128)S(1)}, s32[64]{0:T(128)S(1)}, s32[64]{0:T(128)S(1)}) %tuple.19), branch_computations={%region_4.0_spmd, %region_5.9_spmd} | conditional | flops 135890448 | bytes 13190965 | solution.py:124
  129.7 101.8 %while.13 = (s32[]{:T(128)}, bf16[16,64,512]{2,1,0:T(8,128)(2,1)S(1)}, s32[16]{0:T(128)S(1)}, s32[64]{0:T(128)S(1)}, s32[64]{0:T(128)S(1)}, /*index=5*/bf16[16,5...) while((s32[]{:T(128)}, ...), condition=%wide.wide.region_8.8_spmd, body=%wide.wide.region_6.7_spmd.sunk | while | flops 135889408 | bytes 8988281 | solution.py:117
  129.7 2.6 maximum_bitcast_fusion.4
  132.4 1.9 copy.25
  134.8 0.6 dynamic_slice.17
  135.4 0.6 iota_add_fusion.4
  136.1 2.6 maximum_bitcast_fusion.4
  138.7 1.9 copy.25
  141.1 0.6 dynamic_slice.17
  141.7 0.6 iota_add_fusion.4
  142.5 2.6 maximum_bitcast_fusion.4
  145.1 1.9 copy.25
  147.5 0.6 dynamic_slice.17
  148.1 0.6 iota_add_fusion.4
  148.8 2.6 maximum_bitcast_fusion.4
  151.5 1.9 copy.25
  154.5 0.6 iota_add_fusion.4
  155.2 2.6 maximum_bitcast_fusion.4
  157.8 1.9 copy.25
  160.8 0.6 iota_add_fusion.4
  161.6 2.6 maximum_bitcast_fusion.4
  164.2 1.9 copy.25
  167.2 0.6 iota_add_fusion.4
  167.9 2.6 maximum_bitcast_fusion.4
  170.6 1.9 copy.25
  173.6 0.6 iota_add_fusion.4
  174.3 2.6 maximum_bitcast_fusion.4
  176.9 1.9 copy.25
  179.9 0.6 iota_add_fusion.4
  180.7 2.6 maximum_bitcast_fusion.4
  183.3 1.9 copy.25
  186.3 0.6 iota_add_fusion.4
  187.0 2.6 maximum_bitcast_fusion.4
  189.7 1.9 copy.25
  192.7 0.6 iota_add_fusion.4
  193.4 2.6 maximum_bitcast_fusion.4
  196.0 1.9 copy.25
  199.0 0.6 iota_add_fusion.4
  199.8 2.6 maximum_bitcast_fusion.4
  202.4 1.9 copy.25
  205.4 0.6 iota_add_fusion.4
  206.1 2.6 maximum_bitcast_fusion.4
  208.8 1.9 copy.25
  211.2 0.6 dynamic_slice.17
  211.8 0.6 iota_add_fusion.4
  212.5 2.6 maximum_bitcast_fusion.4
  215.1 1.9 copy.25
  218.1 0.6 iota_add_fusion.4
  218.9 2.6 maximum_bitcast_fusion.4
  221.5 1.9 copy.25
  224.5 0.6 iota_add_fusion.4
  225.2 2.6 maximum_bitcast_fusion.4
  227.9 1.9 copy.25
  230.9 0.6 iota_add_fusion.4
  231.7 1.0 copy-done
  232.7 26.1 %reduce-scatter.2.cloned.1.call-done = bf16[16,8192]{1,0:T(8,128)(2,1)} async-done(((bf16[64,8192]{1,0:T(8,128)(2,1)}), bf16[16,8192]{1,0:T(8,128)(2,1)}) %reduce-scatter.2.cloned.1.call-update) | async-done | bytes 262160 | tf_op jit(solution)/shard_map/reduce_scatter | solution.py:125
  258.8 1.8 convert_element_type.47
  (77 shorter events, 18.5 us)
Async XLA Ops:
  12.4 23.7 %copy-start.2 = (bf16[64,2048]{1,0:T(8,128)(2,1)S(1)}, bf16[64,2048]{1,0:T(8,128)(2,1)}, u32[]{:S(2)}) copy-start(bf16[64,2048]{1,0:T(8,128)(2,1)} %param.11) | copy-start | bytes 786436
  12.4 116.6 %all-to-all-start = ((bf16[128,64,128]{2,1,0:T(8,128)(2,1)}), bf16[128,64,128]{2,1,0:T(8,128)(2,1)}, u32[]{:S(2)}, u32[]{:S(2)}) async-start(bf16[128,64,128]{2,1,0:T(8,128)(2,1)} %stack.2), calls=%async_computation | async-start | bytes 4194304 | tf_op jit(solution)/shard_map/all_to_all | solution.py:16
  36.0 0.7 copy-start.3
  36.0 2.1 copy-start.4
  36.0 222.8 %reduce-scatter.2.cloned.1.call-start = ((), (), s32[]{:S(2)}) async-start(), calls=%async_computation.2 | async-start | bytes 1310720 | tf_op jit(solution)/shard_map/reduce_scatter | solution.py:125
  129.0 0.7 copy-start.1
  231.7 1.0 copy-start
Sparse Core Ops, SparseCore 0:
  232.8 25.9 reduce-scatter.1
